TPU v7x, 32 devices: a whole 2x2x4 slice. The times are simulated.
32 devices in a mesh: row: 4 (over x, core), col: 8 (over z, y).
Axes of the slice: x: 2, y: 2, z: 4, core: 2. Of those that a mesh axis runs over, the one named last changes fastest.
Arguments:
- orbitals: bfloat16 [98304, 4096], P(('row', 'col')), may hold values from -0.09375 to 0.09375
- occupation: int32 [4096], replicated, may hold values from 1 to 128
- owner: int32 [3072, 1], P(('row', 'col')), may hold values from 0 to 7; in each aligned block of 96 rows (0 to 95, 96 to 191, ...) at most 14 rows name the same one
- row_values: bfloat16 [98304, 128], P(('row', 'col')), may hold values from -0.23925781 to 0.23925781
- slab_values: bfloat16 [256, 4096], P(None, ('row', 'col')), may hold values from -6 to 6
- moment_weights: float32 [49, 4096], P(None, ('row', 'col')), may hold values from -0.6 to 0.6
- batch_atom: int32 [32], P(('row', 'col')), may hold values from 0 to 255
- batch_shell: int32 [32], P(('row', 'col')), may hold values from 0 to 63
Outputs:
- density: float32 [4096], P(('row', 'col'))
- moments: float32 [49, 256, 64], P(None, ('row', 'col'))
Inputs may be any that keep to these rules, and one draw needn't show every extreme that they name: Among the 96 blocks of one device no owner is named more than 14 times.
All inputs are finite; a program needn't handle non-finite values.
Results may differ from a plain program's by a relative error of at most 0.0042.
Values may be sent and summed in bfloat16 or wider, within the bound.
No kernel may reach another device: no remote copies, remote signals or barrier semaphores. Data moves between devices by JAX's collectives and lax.ppermute only.
A program may use at most 128 MiB of HBM per device.

v0:
```python
import functools

import jax
import jax.numpy as jnp
from jax import lax
from jax.experimental import pallas as pl
from jax.experimental.pallas import tpu as pltpu
from jax.sharding import PartitionSpec as P


SLAB_DEV = 8
BLK = 32
SHELLS = 64
ATOM_DEV = 8
LMP = 64


def swap(x, axis, mask):
    size = lax.axis_size(axis)
    return lax.ppermute(x, axis, [(i, i ^ mask) for i in range(size)])


def round8(n):
    return -(-n // 8) * 8


def masks_above(size, low):
    out = []
    m = size // 2
    while m >= low:
        out.append(m)
        m //= 2
    return out


VMEM = pl.BlockSpec(memory_space=pltpu.VMEM)
SMEM = pl.BlockSpec(memory_space=pltpu.SMEM)


def weigh(orbitals, occupation):
    def kernel(rows, occ, out):
        weights = occ[...].astype(jnp.float32) / 64.0
        out[...] = (rows[...].astype(jnp.float32) * weights).astype(out.dtype)

    cols = orbitals.shape[1]
    return pl.pallas_call(
        kernel,
        out_shape=jax.ShapeDtypeStruct((SLAB_DEV, cols), jnp.bfloat16),
        in_specs=[VMEM, VMEM],
        out_specs=VMEM,
        compiler_params=pltpu.CompilerParams(vmem_limit_bytes=2**20),
        cost_estimate=pl.CostEstimate(flops=HINT_FLOPS, bytes_accessed=HINT_BYTES, transcendentals=0),
        name="weigh",
    )(orbitals[:SLAB_DEV], occupation.reshape(1, cols))


def plan_kernel(ncol, most, own, slot):
    my_col = lax.axis_index("col")
    for t in range(ncol):
        slot[ncol * most + t] = t * most
    for s in range(ncol * most):
        slot[s] = -1

    def assign(b, c):
        at = ncol * most + (own[b] ^ my_col)
        s = slot[at]
        slot[at] = s + 1
        slot[s] = b
        return c

    lax.fori_loop(0, own.shape[0], assign, 0, unroll=4)


def plan(own, ncol, most):
    return pl.pallas_call(
        functools.partial(plan_kernel, ncol, most),
        out_shape=jax.ShapeDtypeStruct((ncol * most + ncol,), jnp.int32),
        in_specs=[SMEM],
        out_specs=SMEM,
        compiler_params=pltpu.CompilerParams(vmem_limit_bytes=2**20),
        name="plan",
    )(own)


def pack_kernel(slab, mw, packed):
    rows, lm = slab.shape[0], mw.shape[0]
    high = mw[...].astype(jnp.bfloat16)
    low = (mw[...] - high.astype(jnp.float32)).astype(jnp.bfloat16)
    fill = jnp.zeros((round8(lm) - lm, mw.shape[1]), jnp.bfloat16)
    packed[:rows] = slab[...]
    packed[rows:] = jnp.concatenate([high, fill, low, fill], axis=0)


def pack(slab_values, moment_weights):
    rows, points = slab_values.shape
    return pl.pallas_call(
        pack_kernel,
        out_shape=jax.ShapeDtypeStruct((rows + 2 * round8(moment_weights.shape[0]), points), jnp.bfloat16),
        in_specs=[VMEM, VMEM],
        out_specs=VMEM,
        compiler_params=pltpu.CompilerParams(vmem_limit_bytes=2**20),
        name="pack",
    )(slab_values, moment_weights)


HINT_FLOPS = 10**10
HINT_BYTES = 3 * 10**7


def fold_kernel(most, first, slot, orb, phi, out, phit):
    def target(k, c):
        blocks = [slot[(first + k) * most + m] for m in range(most)]
        rows = [pl.ds(pl.multiple_of(jnp.maximum(b, 0) * BLK, BLK), BLK) for b in blocks]
        picked = []
        for b, at in zip(blocks, rows):
            block = phi[at]
            picked.append(jnp.where(b >= 0, block, jnp.zeros_like(block)))
        phit[...] = jnp.concatenate(picked, axis=0).T
        held = jnp.concatenate([orb[at] for at in rows], axis=0)
        acc = jnp.dot(phit[...], held, preferred_element_type=jnp.float32)
        out[k] = acc.astype(out.dtype)
        return c

    lax.fori_loop(0, out.shape[0], target, 0)


def fold(slot, orbitals, row_values, most, first, count):
    cols = orbitals.shape[1]
    points = row_values.shape[1]
    return pl.pallas_call(
        functools.partial(fold_kernel, most, first),
        out_shape=jax.ShapeDtypeStruct((count, points, cols), jnp.bfloat16),
        in_specs=[SMEM, VMEM, VMEM],
        out_specs=VMEM,
        scratch_shapes=[pltpu.VMEM((points, most * BLK), jnp.bfloat16)],
        compiler_params=pltpu.CompilerParams(vmem_limit_bytes=4 * 2**20),
        cost_estimate=pl.CostEstimate(
            flops=2 * count * most * BLK * cols * points,
            bytes_accessed=2 * count * most * BLK * cols,
            transcendentals=0,
        ),
    )(slot, orbitals, row_values)


def body(
    orbitals, occupation, owner, row_values, slab_values, moment_weights, batch_atom, batch_shell
):
    nrow, ncol = lax.axis_size("row"), lax.axis_size("col")
    nblk = owner.shape[0]
    most = nblk // ncol + 2
    lm = moment_weights.shape[0]
    cat = lambda xs: jnp.concatenate(xs, axis=0)
    far = lambda rm, cm, rl: [(r ^ rm, c ^ cm) for r, c in rl]

    mine = weigh(orbitals, occupation)
    local = pack(slab_values, moment_weights)
    slot = plan(owner[:, 0], ncol, most)
    early = ncol // 4
    tables = [
        fold(slot, orbitals, row_values, most, 0, early), fold(slot, orbitals, row_values, most, early, ncol - early)
    ]

    col_high = masks_above(ncol, 2)
    got, rel = [mine], [(0, 0)]
    for m in col_high:
        got = got + [swap(x, "col", m) for x in got]
        rel = rel + far(0, m, rel)
    for m in masks_above(nrow, 4):
        got = got + [swap(x, "row", m) for x in got]
        rel = rel + far(m, 0, rel)
    base = cat(got)
    across = swap(base, "row", 2)
    along = swap(base, "col", 1)
    diag = swap(along, "row", 2)
    n = base.shape[0]
    parts = []
    for k, (x, rl, col0) in enumerate(
        [
            (base, rel, 0),
            (across, far(2, 0, rel), 0),
            (along, far(0, 1, rel), 0),
            (diag, far(2, 1, rel), 0),
        ]
    ):
        row0 = min(k, 3) * n
        parts.append((x, row0, col0, rl))
        parts.append((swap(x, "row", 1), row0 + 4 * n, col0, far(1, 0, rl)))

    vs = [(local, 0)]
    for m in col_high:
        vs = vs + [(swap(y, "col", m), c ^ m) for y, c in vs]
    near = []
    rest = list(vs)
    vs, order = [], []
    for group in (near, rest):
        if group:
            both = cat([y for y, _ in group])
            cms = [c for _, c in group]
            vs += [both, swap(both, "col", 1)]
            order += [cms, [c ^ 1 for c in cms]]

    send = meet(parts, vs, order, tables, batch_atom.reshape(1, 1), batch_shell.reshape(1, 1), nrow, ncol)
    recv = lax.all_to_all(send, ("row", "col"), 0, 0, tiled=True)
    start = (lax.axis_index("row") * ncol + lax.axis_index("col")) * (ATOM_DEV * SHELLS)
    bins = jnp.arange(ATOM_DEV * SHELLS, dtype=jnp.int32).reshape(1, -1) + start
    density, moments = gather_up(recv, bins, lm, nrow, ncol)
    return density.reshape(-1), moments


def gather_up(recv, bins, lm, nrow, ncol):
    points = recv.shape[2]
    pm_rows = ncol // 2

    def kernel(got, bins, density, moments):
        my_row = lax.axis_index("row")
        total = got[my_row * ncol]
        for c in range(1, ncol):
            total = total + got[my_row * ncol + c]
        density[...] = total[pm_rows : pm_rows + 1]
        left, right = [], []
        for r in range(nrow):
            acc = got[r * ncol, :pm_rows]
            for c in range(1, ncol):
                acc = acc + got[r * ncol + c, :pm_rows]
            left.append(acc[:, :LMP])
            right.append(acc[:, LMP:])
        low = cat0([got[r * ncol + t, pm_rows + 1 : pm_rows + 2] for r in range(nrow) for t in range(pm_rows)])
        high = cat0(
            [got[r * ncol + pm_rows + t, pm_rows + 1 : pm_rows + 2] for r in range(nrow) for t in range(pm_rows)]
        )
        pm = cat0(left + right)
        bin_of = cat0([low, high]).astype(jnp.int32)
        width = bin_of.shape[1]
        hot = jnp.concatenate(
            [
                (bin_of == bins[:, k : k + width]).astype(jnp.float32)
                for k in range(0, bins.shape[1], width)
            ],
            axis=1,
        )
        placed = lax.dot_general(
            pm,
            hot,
            (((0,), (0,)), ((), ())),
            precision=lax.Precision.HIGHEST,
            preferred_element_type=jnp.float32,
        )
        for a in range(ATOM_DEV):
            moments[:, a, :] = placed[:lm, a * SHELLS : (a + 1) * SHELLS]

    return pl.pallas_call(
        kernel,
        out_shape=[
            jax.ShapeDtypeStruct((1, points), jnp.float32),
            jax.ShapeDtypeStruct((lm, ATOM_DEV, SHELLS), jnp.float32),
        ],
        in_specs=[VMEM, VMEM],
        out_specs=[VMEM, VMEM],
        compiler_params=pltpu.CompilerParams(vmem_limit_bytes=4 * 2**20),
        name="gather_up",
    )(recv, bins)


def cat0(xs):
    return jnp.concatenate(xs, axis=0)


def meet(parts, vs, order, tables, atom, shell, nrow, ncol):
    points, cols = tables[0].shape[1:]
    early = tables[0].shape[0]
    places = [(row0, col0) for _, row0, col0, _ in parts]
    pieces = [x for x, *_ in parts]
    slab = max(row0 + x.shape[0] for x, row0, *_ in parts)
    pm_rows = ncol // 2
    out_rows = round8(pm_rows + 2)
    pair = 2
    rel_of = {}
    for x, row0, _, rl in parts:
        for i, r in enumerate(rl):
            rel_of[row0 // SLAB_DEV + i] = r
    part = (vs[0].shape[0] // len(order[0]) - slab) // 2
    vrows = slab + 2 * part
    nv = len(vs)

    def kernel(*refs):
        piece_refs = refs[: len(pieces)]
        v_refs = refs[len(pieces) : len(pieces) + nv]
        atom_ref, shell_ref, c_low, c_high, out, wt, vf, terms = refs[len(pieces) + nv :]
        where = {cm: (v_refs[a], k * vrows) for a, cms in enumerate(order) for k, cm in enumerate(cms)}
        my_row, my_col = lax.axis_index("row"), lax.axis_index("col")
        for ref, (row0, col0) in zip(piece_refs, places):
            wt[row0 : row0 + ref.shape[0], col0 : col0 + ref.shape[1]] = ref[...]
        for cm in range(ncol):
            ref, at = where[cm]
            vf[cm] = ref[at : at + slab].astype(jnp.float32).reshape(slab // SLAB_DEV, SLAB_DEV, points)

        def targets(c_ref, at, first, many):
            two = lax.dot_general(
                wt[...],
                c_ref[pl.ds(at, many)].reshape(many * points, cols),
                (((1,), (1,)), ((), ())),
                preferred_element_type=jnp.float32,
            )
            for q in range(many):
                acc = jnp.zeros((SLAB_DEV, points), jnp.float32)
                for i, (rm, cm) in rel_of.items():
                    dev = (my_row ^ rm) * ncol + (my_col ^ cm)
                    acc += (
                        two[i * SLAB_DEV : (i + 1) * SLAB_DEV, q * points : (q + 1) * points]
                        * vf[first + q, dev]
                    )
                terms[first + q] = jnp.sum(acc, axis=0, keepdims=True)

        for c_ref, base in ((c_low, 0), (c_high, early)):
            count = c_ref.shape[0]
            if ncol <= 8:
                for at in range(0, count, pair):
                    targets(c_ref, at, base + at, min(pair, count - at))
            else:

                def both(g, c, c_ref=c_ref, base=base):
                    targets(c_ref, g * pair, base + g * pair, pair)
                    return c

                lax.fori_loop(0, count // pair, both, 0)

        lhs_parts = []
        rhs_parts = []
        row_id = lax.broadcasted_iota(jnp.int32, (pm_rows, points), 0)
        for cm in range(ncol):
            t = my_col ^ cm
            ref, at = where[cm]
            mw = ref[at + slab : at + slab + part].astype(jnp.float32)
            mw = mw + ref[at + slab + part : at + vrows].astype(jnp.float32)
            mw = jnp.concatenate([mw, jnp.zeros((LMP - part, points), jnp.float32)], axis=0)
            lhs_parts.append(jnp.where(row_id == t % pm_rows, terms[cm], 0.0))
            low = t < pm_rows
            rhs_parts.append(jnp.concatenate([jnp.where(low, mw, 0.0), jnp.where(low, 0.0, mw)], axis=0))
        pm = lax.dot_general(
            jnp.concatenate(lhs_parts, axis=1),
            jnp.concatenate(rhs_parts, axis=1),
            (((1,), (1,)), ((), ())),
            precision=lax.Precision.HIGHEST,
            preferred_element_type=jnp.float32,
        )
        own_bin = (atom_ref[...] * SHELLS + shell_ref[...]).astype(jnp.float32)
        tail = jnp.broadcast_to(own_bin, (1, points))
        fill = jnp.zeros((out_rows - pm_rows - 2, points), jnp.float32)
        for cm in range(ncol):
            t = my_col ^ cm
            block = jnp.concatenate([pm, terms[cm], tail, fill], axis=0)
            for r in range(nrow):
                out[r * ncol + t] = block

    return pl.pallas_call(
        kernel,
        out_shape=jax.ShapeDtypeStruct((nrow * ncol, out_rows, points), jnp.float32),
        in_specs=[VMEM] * (len(pieces) + nv + 4),
        out_specs=VMEM,
        scratch_shapes=[
            pltpu.VMEM((slab, cols), jnp.bfloat16),
            pltpu.VMEM((ncol, slab // SLAB_DEV, SLAB_DEV, points), jnp.float32),
            pltpu.VMEM((ncol, 1, points), jnp.float32),
        ],
        compiler_params=pltpu.CompilerParams(vmem_limit_bytes=8 * 2**20 if slab <= 256 else 40 * 2**20),
        cost_estimate=pl.CostEstimate(
            flops=2 * slab * cols * ncol * points, bytes_accessed=2 * ncol * points * cols, transcendentals=0
        ),
        name="meet",
    )(*pieces, *vs, atom, shell, *tables)


def solution(mesh):
    placed = (
        P(("row", "col"), None),
        P(),
        P(("row", "col"), None),
        P(("row", "col"), None),
        P(None, ("row", "col")),
        P(None, ("row", "col")),
        P(("row", "col")),
        P(("row", "col")),
    )
    return jax.shard_map(
        body,
        mesh=mesh,
        in_specs=placed,
        out_specs=(P(("row", "col")), P(None, ("row", "col"), None)),
        check_vma=False,
    )
```

profile of v0, /device:TPU:0, one launch (start us, length us, event | category | flops | bytes accessed | tf_op | source)
XLA Modules:
  0.0 57.2 jit_solution(7382073558454375804)
XLA Ops:
  0.6 0.8 %slice.3.rows = bf16[8,4096]{1,0:T(8,128)(2,1)S(1)} slice(bf16[3072,4096]{1,0:T(8,128)(2,1)} %orb.3), slice={[0:8], [0:4096]} | slice | bytes 131072 | tf_op jit(solution)/shard_map/slice | solution.py:54
  1.5 0.7 %copy-done.4 = s32[4096]{0:T(1024)S(1)} copy-done((s32[4096]{0:T(1024)S(1)}, s32[4096]{0:T(1024)}, u32[]{:S(2)}) %copy-start.4) | copy-done | bytes 16408
  2.2 4.1 %collective-permute-start = (bf16[8,4096]{1,0:T(8,128)(2,1)S(1)}, bf16[8,4096]{1,0:T(8,128)(2,1)S(1)}, u32[]{:S(2)}, u32[]{:S(2)}) collective-permute-start(bf16[8,4096]{1,0:T(8,128)(2,1)S(1)} %weigh.1), channel_id=1, source_target_pairs={{0,4},{1,5},{2,6},{3,7},{4,0},{5,1},{6,2},{7,3},{8,12},{9,13},{10,... | collective-permute-start | bytes 196616 | tf_op jit(solution)/shard_map/ppermute | solution.py:20
  6.4 1.6 %collective-permute-start.1 = (bf16[8,4096]{1,0:T(8,128)(2,1)S(1)}, bf16[8,4096]{1,0:T(8,128)(2,1)S(1)}, u32[]{:S(2)}, u32[]{:S(2)}) collective-permute-start(bf16[8,4096]{1,0:T(8,128)(2,1)S(1)} %weigh.1), channel_id=1, source_target_pairs={{0,2},{1,3},{2,0},{3,1},{4,6},{5,7},{6,4},{7,5},{8,10},{9,11},{10,... | collective-permute-start | bytes 196616 | tf_op jit(solution)/shard_map/ppermute | solution.py:20
  8.0 1.5 %collective-permute-done = bf16[8,4096]{1,0:T(8,128)(2,1)S(1)} collective-permute-done((bf16[8,4096]{1,0:T(8,128)(2,1)S(1)}, bf16[8,4096]{1,0:T(8,128)(2,1)S(1)}, u32[]{:S(2)}, u32[]{:S(2)}) %collective-permute-start) | collective-permute-done | bytes 65568 | tf_op jit(solution)/shard_map/ppermute | solution.py:20
  9.4 1.4 %collective-permute-start.2 = (bf16[8,4096]{1,0:T(8,128)(2,1)S(1)}, bf16[8,4096]{1,0:T(8,128)(2,1)S(1)}, u32[]{:S(2)}, u32[]{:S(2)}) collective-permute-start(bf16[8,4096]{1,0:T(8,128)(2,1)S(1)} %collective-permute-done), channel_id=1, source_target_pairs={{0,2},{1,3},{2,0},{3,1},{4,6},{5,7},{6,4},{7,5},{8,10},{9,11},{10,... | collective-permute-start | bytes 196616 | tf_op jit(solution)/shard_map/ppermute | solution.py:20
  10.8 2.9 %collective-permute-done.2 = bf16[8,4096]{1,0:T(8,128)(2,1)S(1)} collective-permute-done((bf16[8,4096]{1,0:T(8,128)(2,1)S(1)}, bf16[8,4096]{1,0:T(8,128)(2,1)S(1)}, u32[]{:S(2)}, u32[]{:S(2)}) %collective-permute-start.2) | collective-permute-done | bytes 65568 | tf_op jit(solution)/shard_map/ppermute | solution.py:20
  13.7 2.0 %collective-permute-start.6 = (bf16[32,4096]{1,0:T(8,128)(2,1)S(1)}, bf16[32,4096]{1,0:T(8,128)(2,1)S(1)}, u32[]{:S(2)}, u32[]{:S(2)}) collective-permute-start(bf16[32,4096]{1,0:T(8,128)(2,1)S(1)} %pad_maximum_fusion.1.refs_0_), channel_id=1, source_target_pairs={{0,1},{1,0},{2,3},{3,2},{4,5},{5,4},{6,7},{7,6},{8,9},{9,8},{10,11... | collective-permute-start | bytes 786440 | tf_op jit(solution)/shard_map/ppermute | solution.py:20
  15.7 2.3 %collective-permute-start.10 = (bf16[368,128]{1,0:T(8,128)(2,1)S(1)}, bf16[368,128]{1,0:T(8,128)(2,1)S(1)}, u32[]{:S(2)}, u32[]{:S(2)}) collective-permute-start(bf16[368,128]{1,0:T(8,128)(2,1)S(1)} %pack.1), channel_id=1, source_target_pairs={{0,4},{1,5},{2,6},{3,7},{4,0},{5,1},{6,2},{7,3},{8,12},{9,13},{10,... | collective-permute-start | bytes 282632 | tf_op jit(solution)/shard_map/ppermute | solution.py:20
  18.0 1.9 %collective-permute-start.11 = (bf16[368,128]{1,0:T(8,128)(2,1)S(1)}, bf16[368,128]{1,0:T(8,128)(2,1)S(1)}, u32[]{:S(2)}, u32[]{:S(2)}) collective-permute-start(bf16[368,128]{1,0:T(8,128)(2,1)S(1)} %pack.1), channel_id=1, source_target_pairs={{0,2},{1,3},{2,0},{3,1},{4,6},{5,7},{6,4},{7,5},{8,10},{9,11},{10,... | collective-permute-start | bytes 282632 | tf_op jit(solution)/shard_map/ppermute | solution.py:20
  19.9 2.4 %collective-permute-done.10 = bf16[368,128]{1,0:T(8,128)(2,1)S(1)} collective-permute-done((bf16[368,128]{1,0:T(8,128)(2,1)S(1)}, bf16[368,128]{1,0:T(8,128)(2,1)S(1)}, u32[]{:S(2)}, u32[]{:S(2)}) %collective-permute-start.10) | collective-permute-done | bytes 94240 | tf_op jit(solution)/shard_map/ppermute | solution.py:20
  22.3 0.3 collective-permute-start.12
  22.6 1.5 %collective-permute-start.4 = (bf16[32,4096]{1,0:T(8,128)(2,1)S(1)}, bf16[32,4096]{1,0:T(8,128)(2,1)S(1)}, u32[]{:S(2)}, u32[]{:S(2)}) collective-permute-start(bf16[32,4096]{1,0:T(8,128)(2,1)S(1)} %pad_maximum_fusion.1.refs_0_), channel_id=1, source_target_pairs={{0,16},{8,24},{16,0},{24,8},{1,17},{9,25},{17,1},{25,9},{2,18},{10... | collective-permute-start | bytes 786440 | tf_op jit(solution)/shard_map/ppermute | solution.py:20
  24.1 0.5 collective-permute-start.8
  24.6 2.3 %collective-permute-done.12 = bf16[368,128]{1,0:T(8,128)(2,1)S(1)} collective-permute-done((bf16[368,128]{1,0:T(8,128)(2,1)S(1)}, bf16[368,128]{1,0:T(8,128)(2,1)S(1)}, u32[]{:S(2)}, u32[]{:S(2)}) %collective-permute-start.12) | collective-permute-done | bytes 94240 | tf_op jit(solution)/shard_map/ppermute | solution.py:20
  27.0 1.8 %plan.1.slot = s32[120]{0:T(128)S(1)} custom-call(s32[96]{0:T(128)S(1)} %bitcast.8), custom_call_target="tpu_custom_call" | custom-call | tf_op jit(solution)/shard_map/plan/pallas_call | solution.py:75
  30.1 2.1 %shard_map.95.refs_12_ = bf16[2,128,4096]{2,1,0:T(8,128)(2,1)S(1)} custom-call(s32[120]{0:T(128)S(1)} %plan.1.slot, bf16[3072,4096]{1,0:T(8,128)(2,1)S(1)} %copy-done, bf16[3072,128]{1,0:T(8,128)(2,1)S(1)} %copy-done.1), custom_call_target="tpu_custom_call" | custom-call | flops 939524096 | bytes 7340032 | tf_op jit(solution)/shard_map/pallas_call | solution.py:130
  32.3 0.5 collective-permute-start.7
  32.9 0.8 %collective-permute-done.8.refs_6_ = bf16[32,4096]{1,0:T(8,128)(2,1)S(1)} collective-permute-done((bf16[32,4096]{1,0:T(8,128)(2,1)S(1)}, bf16[32,4096]{1,0:T(8,128)(2,1)S(1)}, u32[]{:S(2)}, u32[]{:S(2)}) %collective-permute-start.8) | collective-permute-done | bytes 262176 | tf_op jit(solution)/shard_map/ppermute | solution.py:20
  33.7 5.1 %shard_map.96.refs_13_ = bf16[6,128,4096]{2,1,0:T(8,128)(2,1)S(1)} custom-call(s32[120]{0:T(128)S(1)} %plan.1.slot, bf16[3072,4096]{1,0:T(8,128)(2,1)S(1)} %copy-done, bf16[3072,128]{1,0:T(8,128)(2,1)S(1)} %copy-done.1), custom_call_target="tpu_custom_call" | custom-call | flops 2818572288 | bytes 22020096 | tf_op jit(solution)/shard_map/pallas_call | solution.py:130
  38.9 3.7 %meet.1 = f32[32,8,128]{2,1,0:T(8,128)} custom-call(bf16[32,4096]{1,0:T(8,128)(2,1)S(1)} %pad_maximum_fusion.1.refs_0_, bf16[32,4096]{1,0:T(8,128)(2,1)S(1)} %collective-permute-done.3.refs_1_, bf16[32,4096]{1,0:T(8,128)(2,1)S(1)} %collective-permute-done.4.refs_2_, bf16[32,4096]{1,0:T(8,128)(2,1)S(1)} %collective-permute-done.5.refs_3_, ...), custom_call_target="tpu_custom_call" | custom-call | flops 2147483648 | bytes 8388608 | tf_op jit(solution)/shard_map/meet/pallas_call | solution.py:355
  42.6 5.4 %all-to-all-start = ((f32[32,8,128]{2,1,0:T(8,128)}), f32[32,8,128]{2,1,0:T(8,128)S(1)}, u32[]{:S(2)}, u32[]{:S(2)}) async-start(f32[32,8,128]{2,1,0:T(8,128)} %meet.1), calls=%async_computation | async-start | bytes 262144 | tf_op jit(solution)/shard_map/all_to_all | solution.py:203
  48.1 7.8 %all-to-all-done.got = f32[32,8,128]{2,1,0:T(8,128)S(1)} async-done(((f32[32,8,128]{2,1,0:T(8,128)}), f32[32,8,128]{2,1,0:T(8,128)S(1)}, u32[]{:S(2)}, u32[]{:S(2)}) %all-to-all-start) | async-done | bytes 131104 | tf_op jit(solution)/shard_map/all_to_all | solution.py:203
  55.8 1.4 %gather_up.1 = (f32[1,128]{1,0:T(1,128)}, f32[49,8,64]{2,1,0:T(8,128)}) custom-call(f32[32,8,128]{2,1,0:T(8,128)S(1)} %all-to-all-done.got, s32[1,512]{1,0:T(1,128)S(1)} %iota_add_fusion.bins), custom_call_target="tpu_custom_call" | custom-call | tf_op jit(solution)/shard_map/gather_up/pallas_call | solution.py:251
  (29 shorter events, 0.4 us)
Async XLA Ops:
  1.5 0.7 %copy-start.4 = (s32[4096]{0:T(1024)S(1)}, s32[4096]{0:T(1024)}, u32[]{:S(2)}) copy-start(s32[4096]{0:T(1024)} %param.9) | copy-start | bytes 49156
  2.2 13.5 %copy-start.2 = (bf16[256,128]{1,0:T(8,128)(2,1)S(1)}, bf16[256,128]{1,0:T(8,128)(2,1)}, u32[]{:S(2)}) copy-start(bf16[256,128]{1,0:T(8,128)(2,1)} %slab.1) | copy-start | bytes 196612
  2.2 13.5 %copy-start.3 = (f32[49,128]{1,0:T(8,128)S(1)}, f32[49,128]{1,0:T(8,128)}, u32[]{:S(2)}) copy-start(f32[49,128]{1,0:T(8,128)} %mw.1) | copy-start | bytes 75268
  2.2 24.8 %copy-start.5 = (s32[96,1]{0,1:T(1,128)S(1)}, s32[96,1]{0,1:T(1,128)}, u32[]{:S(2)}) copy-start(s32[96,1]{0,1:T(1,128)} %param.10) | copy-start | bytes 1156
  2.2 27.9 %copy-start = (bf16[3072,4096]{1,0:T(8,128)(2,1)S(1)}, bf16[3072,4096]{1,0:T(8,128)(2,1)}, u32[]{:S(2)}) copy-start(bf16[3072,4096]{1,0:T(8,128)(2,1)} %orb.3) | copy-start | bytes 75497472
  2.2 27.9 %copy-start.1 = (bf16[3072,128]{1,0:T(8,128)(2,1)S(1)}, bf16[3072,128]{1,0:T(8,128)(2,1)}, u32[]{:S(2)}) copy-start(bf16[3072,128]{1,0:T(8,128)(2,1)} %phi.3) | copy-start | bytes 2359300
  2.2 7.2 %collective-permute-start = (bf16[8,4096]{1,0:T(8,128)(2,1)S(1)}, bf16[8,4096]{1,0:T(8,128)(2,1)S(1)}, u32[]{:S(2)}, u32[]{:S(2)}) collective-permute-start(bf16[8,4096]{1,0:T(8,128)(2,1)S(1)} %weigh.1), channel_id=1, source_target_pairs={{0,4},{1,5},{2,6},{3,7},{4,0},{5,1},{6,2},{7,3},{8,12},{9,13},{10,... | collective-permute-start | bytes 196616 | tf_op jit(solution)/shard_map/ppermute | solution.py:20
  6.4 4.4 %collective-permute-start.1 = (bf16[8,4096]{1,0:T(8,128)(2,1)S(1)}, bf16[8,4096]{1,0:T(8,128)(2,1)S(1)}, u32[]{:S(2)}, u32[]{:S(2)}) collective-permute-start(bf16[8,4096]{1,0:T(8,128)(2,1)S(1)} %weigh.1), channel_id=1, source_target_pairs={{0,2},{1,3},{2,0},{3,1},{4,6},{5,7},{6,4},{7,5},{8,10},{9,11},{10,... | collective-permute-start | bytes 196616 | tf_op jit(solution)/shard_map/ppermute | solution.py:20
  9.4 4.3 %collective-permute-start.2 = (bf16[8,4096]{1,0:T(8,128)(2,1)S(1)}, bf16[8,4096]{1,0:T(8,128)(2,1)S(1)}, u32[]{:S(2)}, u32[]{:S(2)}) collective-permute-start(bf16[8,4096]{1,0:T(8,128)(2,1)S(1)} %collective-permute-done), channel_id=1, source_target_pairs={{0,2},{1,3},{2,0},{3,1},{4,6},{5,7},{6,4},{7,5},{8,10},{9,11},{10,... | collective-permute-start | bytes 196616 | tf_op jit(solution)/shard_map/ppermute | solution.py:20
  13.7 10.4 %collective-permute-start.6 = (bf16[32,4096]{1,0:T(8,128)(2,1)S(1)}, bf16[32,4096]{1,0:T(8,128)(2,1)S(1)}, u32[]{:S(2)}, u32[]{:S(2)}) collective-permute-start(bf16[32,4096]{1,0:T(8,128)(2,1)S(1)} %pad_maximum_fusion.1.refs_0_), channel_id=1, source_target_pairs={{0,1},{1,0},{2,3},{3,2},{4,5},{5,4},{6,7},{7,6},{8,9},{9,8},{10,11... | collective-permute-start | bytes 786440 | tf_op jit(solution)/shard_map/ppermute | solution.py:20
  15.7 6.6 %collective-permute-start.10 = (bf16[368,128]{1,0:T(8,128)(2,1)S(1)}, bf16[368,128]{1,0:T(8,128)(2,1)S(1)}, u32[]{:S(2)}, u32[]{:S(2)}) collective-permute-start(bf16[368,128]{1,0:T(8,128)(2,1)S(1)} %pack.1), channel_id=1, source_target_pairs={{0,4},{1,5},{2,6},{3,7},{4,0},{5,1},{6,2},{7,3},{8,12},{9,13},{10,... | collective-permute-start | bytes 282632 | tf_op jit(solution)/shard_map/ppermute | solution.py:20
  18.0 6.6 %collective-permute-start.11 = (bf16[368,128]{1,0:T(8,128)(2,1)S(1)}, bf16[368,128]{1,0:T(8,128)(2,1)S(1)}, u32[]{:S(2)}, u32[]{:S(2)}) collective-permute-start(bf16[368,128]{1,0:T(8,128)(2,1)S(1)} %pack.1), channel_id=1, source_target_pairs={{0,2},{1,3},{2,0},{3,1},{4,6},{5,7},{6,4},{7,5},{8,10},{9,11},{10,... | collective-permute-start | bytes 282632 | tf_op jit(solution)/shard_map/ppermute | solution.py:20
  22.3 4.6 %collective-permute-start.12 = (bf16[368,128]{1,0:T(8,128)(2,1)S(1)}, bf16[368,128]{1,0:T(8,128)(2,1)S(1)}, u32[]{:S(2)}, u32[]{:S(2)}) collective-permute-start(bf16[368,128]{1,0:T(8,128)(2,1)S(1)} %collective-permute-done.10), channel_id=1, source_target_pairs={{0,2},{1,3},{2,0},{3,1},{4,6},{5,7},{6,4},{7,5},{8,10},{9,11},{10,... | collective-permute-start | bytes 282632 | tf_op jit(solution)/shard_map/ppermute | solution.py:20
  22.6 10.2 %collective-permute-start.4 = (bf16[32,4096]{1,0:T(8,128)(2,1)S(1)}, bf16[32,4096]{1,0:T(8,128)(2,1)S(1)}, u32[]{:S(2)}, u32[]{:S(2)}) collective-permute-start(bf16[32,4096]{1,0:T(8,128)(2,1)S(1)} %pad_maximum_fusion.1.refs_0_), channel_id=1, source_target_pairs={{0,16},{8,24},{16,0},{24,8},{1,17},{9,25},{17,1},{25,9},{2,18},{10... | collective-permute-start | bytes 786440 | tf_op jit(solution)/shard_map/ppermute | solution.py:20
  24.1 9.6 %collective-permute-start.8 = (bf16[32,4096]{1,0:T(8,128)(2,1)S(1)}, bf16[32,4096]{1,0:T(8,128)(2,1)S(1)}, u32[]{:S(2)}, u32[]{:S(2)}) collective-permute-start(bf16[32,4096]{1,0:T(8,128)(2,1)S(1)} %collective-permute-done.6.refs_4_), channel_id=1, source_target_pairs={{0,16},{8,24},{16,0},{24,8},{1,17},{9,25},{17,1},{25,9},{2,18},{10... | collective-permute-start | bytes 786440 | tf_op jit(solution)/shard_map/ppermute | solution.py:20
  26.9 11.9 %collective-permute-start.13 = (bf16[1472,128]{1,0:T(8,128)(2,1)S(1)}, bf16[1472,128]{1,0:T(8,128)(2,1)S(1)}, u32[]{:S(2)}, u32[]{:S(2)}) collective-permute-start(bf16[1472,128]{1,0:T(8,128)(2,1)S(1)} %pad_maximum_fusion.refs_8_), channel_id=1, source_target_pairs={{0,1},{1,0},{2,3},{3,2},{4,5},{5,4},{6,7},{7,6},{8,9},{9,8},{10,11... | collective-permute-start | bytes 1130504 | tf_op jit(solution)/shard_map/ppermute | solution.py:20
  32.2 6.6 %collective-permute-start.3 = (bf16[32,4096]{1,0:T(8,128)(2,1)S(1)}, bf16[32,4096]{1,0:T(8,128)(2,1)S(1)}, u32[]{:S(2)}, u32[]{:S(2)}) collective-permute-start(bf16[32,4096]{1,0:T(8,128)(2,1)S(1)} %pad_maximum_fusion.1.refs_0_), channel_id=1, source_target_pairs={{0,8},{8,0},{16,24},{24,16},{1,9},{9,1},{17,25},{25,17},{2,10},{10... | collective-permute-start | bytes 786440 | tf_op jit(solution)/shard_map/ppermute | solution.py:20
  32.3 6.6 %collective-permute-start.7 = (bf16[32,4096]{1,0:T(8,128)(2,1)S(1)}, bf16[32,4096]{1,0:T(8,128)(2,1)S(1)}, u32[]{:S(2)}, u32[]{:S(2)}) collective-permute-start(bf16[32,4096]{1,0:T(8,128)(2,1)S(1)} %collective-permute-done.6.refs_4_), channel_id=1, source_target_pairs={{0,8},{8,0},{16,24},{24,16},{1,9},{9,1},{17,25},{25,17},{2,10},{10... | collective-permute-start | bytes 786440 | tf_op jit(solution)/shard_map/ppermute | solution.py:20
  32.8 6.1 %collective-permute-start.5 = (bf16[32,4096]{1,0:T(8,128)(2,1)S(1)}, bf16[32,4096]{1,0:T(8,128)(2,1)S(1)}, u32[]{:S(2)}, u32[]{:S(2)}) collective-permute-start(bf16[32,4096]{1,0:T(8,128)(2,1)S(1)} %collective-permute-done.4.refs_2_), channel_id=1, source_target_pairs={{0,8},{8,0},{16,24},{24,16},{1,9},{9,1},{17,25},{25,17},{2,10},{10... | collective-permute-start | bytes 786440 | tf_op jit(solution)/shard_map/ppermute | solution.py:20
  33.7 5.2 %collective-permute-start.9 = (bf16[32,4096]{1,0:T(8,128)(2,1)S(1)}, bf16[32,4096]{1,0:T(8,128)(2,1)S(1)}, u32[]{:S(2)}, u32[]{:S(2)}) collective-permute-start(bf16[32,4096]{1,0:T(8,128)(2,1)S(1)} %collective-permute-done.8.refs_6_), channel_id=1, source_target_pairs={{0,8},{8,0},{16,24},{24,16},{1,9},{9,1},{17,25},{25,17},{2,10},{10... | collective-permute-start | bytes 786440 | tf_op jit(solution)/shard_map/ppermute | solution.py:20
  42.6 13.2 %all-to-all-start = ((f32[32,8,128]{2,1,0:T(8,128)}), f32[32,8,128]{2,1,0:T(8,128)S(1)}, u32[]{:S(2)}, u32[]{:S(2)}) async-start(f32[32,8,128]{2,1,0:T(8,128)} %meet.1), calls=%async_computation | async-start | bytes 262144 | tf_op jit(solution)/shard_map/all_to_all | solution.py:203
where the time goes:
time: 57.5 us; the launch traced here: 57.2 us
  starting transfers between devices  21.7 us (38%)
  waiting for transfers between devices  17.7 us (31%)
  Pallas kernels  14.1 us (25%)
  between operations  2.09 us (4%)
  local copies, waits for them, and re-layouts  1.59 us (3%)
    ppermute x14, starting transfers between devices, swap(): return lax.ppermute(x, axis, [(i, i ^ mask) for i in range(size)])  16.3 us
    ppermute x14, waiting for transfers between devices, swap(): return lax.ppermute(x, axis, [(i, i ^ mask) for i in range(size)])  9.91 us
    all_to_all x1, waiting for transfers between devices, body(): recv = lax.all_to_all(send, ('row', 'col'), 0, 0, tiled=True)  7.79 us
    pallas_call x2, Pallas kernels, fold(): pl.pallas_call(functools.partial(fold_kernel, most, first), out_shape=jax...  7.19 us
    all_to_all x1, starting transfers between devices, body(): recv = lax.all_to_all(send, ('row', 'col'), 0, 0, tiled=True)  5.39 us
    pallas_call x1, Pallas kernels, meet(): pl.pallas_call(kernel, out_shape=jax.ShapeDtypeStruct((nrow * ncol, out_r...  3.75 us
    pallas_call x1, Pallas kernels, plan(): pl.pallas_call(functools.partial(plan_kernel, ncol, most), out_shape=jax....  1.75 us
    pallas_call x1, Pallas kernels, gather_up(): pl.pallas_call(kernel, out_shape=[jax.ShapeDtypeStruct((1, points), jnp.f...  1.39 us
  transfers between devices with their start and end apart: 15, of which 6 were waited for; matrix products, arithmetic and copies ran while one was open for 0% of the time, Pallas kernels for 16%

commit v1 on v0

--- a/solution.py
+++ b/solution.py
@@ -168,23 +168,25 @@
     for m in masks_above(nrow, 4):
         got = got + [swap(x, "row", m) for x in got]
         rel = rel + far(m, 0, rel)
+    own_y = swap(mine, "col", 1)
     base = cat(got)
+    others = cat(got[1:])
     across = swap(base, "row", 2)
-    along = swap(base, "col", 1)
+    along = swap(others, "col", 1)
+    first = cat([own_y, swap(own_y, "row", 2)])
     diag = swap(along, "row", 2)
-    n = base.shape[0]
-    parts = []
-    for k, (x, rl, col0) in enumerate(
-        [
-            (base, rel, 0),
-            (across, far(2, 0, rel), 0),
-            (along, far(0, 1, rel), 0),
-            (diag, far(2, 1, rel), 0),
-        ]
-    ):
-        row0 = min(k, 3) * n
-        parts.append((x, row0, col0, rl))
-        parts.append((swap(x, "row", 1), row0 + 4 * n, col0, far(1, 0, rl)))
+    parts, row0 = [], 0
+    for x, rl in [
+        (base, rel),
+        (across, far(2, 0, rel)),
+        (first, [(0, 1), (2, 1)]),
+        (along, far(0, 1, rel[1:])),
+        (diag, far(2, 1, rel[1:])),
+    ]:
+        n = x.shape[0]
+        parts.append((x, row0, 0, rl))
+        parts.append((swap(x, "row", 1), row0 + n, 0, far(1, 0, rl)))
+        row0 += 2 * n
 
     vs = [(local, 0)]
     for m in col_high:

time: 57.5 us -> 55.7 us (0.969)
  starting transfers between devices: 21.7 us -> 20 us
    all_to_all x1, starting transfers between devices: 5.39 us -> 4.26 us  [body(): recv = lax.all_to_all(send, ('row', 'col'), 0, 0, tiled=True)]
    ppermute x14 -> x17, starting transfers between devices: 16.3 us -> 15.7 us  [swap(): return lax.ppermute(x, axis, [(i, i ^ mask) for i in range(size)])]
    ppermute x14 -> x17, waiting for transfers between devices: 9.91 us -> 9.72 us  [swap(): return lax.ppermute(x, axis, [(i, i ^ mask) for i in range(size)])]
  transfers between devices with their start and end apart: 15 -> 18, of which waited for: 6 -> 4; matrix products, arithmetic and copies ran while one was open for 0% -> 0% of each run, Pallas kernels for 16% -> 16%
where the time goes in v1:
time: 55.7 us; the launch traced here: 55.4 us
  starting transfers between devices  20 us (36%)
  waiting for transfers between devices  17.5 us (31%)
  Pallas kernels  14.1 us (25%)
  between operations  2.11 us (4%)
  local copies, waits for them, and re-layouts  1.6 us (3%)
    ppermute x17, starting transfers between devices, swap(): return lax.ppermute(x, axis, [(i, i ^ mask) for i in range(size)])  15.7 us
    ppermute x17, waiting for transfers between devices, swap(): return lax.ppermute(x, axis, [(i, i ^ mask) for i in range(size)])  9.72 us
    all_to_all x1, waiting for transfers between devices, body(): recv = lax.all_to_all(send, ('row', 'col'), 0, 0, tiled=True)  7.79 us
    pallas_call x2, Pallas kernels, fold(): pl.pallas_call(functools.partial(fold_kernel, most, first), out_shape=jax...  7.19 us
    all_to_all x1, starting transfers between devices, body(): recv = lax.all_to_all(send, ('row', 'col'), 0, 0, tiled=True)  4.26 us
    pallas_call x1, Pallas kernels, meet(): pl.pallas_call(kernel, out_shape=jax.ShapeDtypeStruct((nrow * ncol, out_r...  3.72 us
    pallas_call x1, Pallas kernels, plan(): pl.pallas_call(functools.partial(plan_kernel, ncol, most), out_shape=jax....  1.75 us
    pallas_call x1, Pallas kernels, gather_up(): pl.pallas_call(kernel, out_shape=[jax.ShapeDtypeStruct((1, points), jnp.f...  1.39 us
  transfers between devices with their start and end apart: 18, of which 4 were waited for; matrix products, arithmetic and copies ran while one was open for 0% of the time, Pallas kernels for 16%

profile of v1, /device:TPU:0, one launch (start us, length us, event | category | flops | bytes accessed | tf_op | source)
XLA Modules:
  0.0 55.4 jit_solution(8512290865278917861)
XLA Ops:
  0.6 0.8 %slice.3.rows = bf16[8,4096]{1,0:T(8,128)(2,1)S(1)} slice(bf16[3072,4096]{1,0:T(8,128)(2,1)} %orb.3), slice={[0:8], [0:4096]} | slice | bytes 131072 | tf_op jit(solution)/shard_map/slice | solution.py:54
  1.5 0.7 %copy-done.4 = s32[4096]{0:T(1024)S(1)} copy-done((s32[4096]{0:T(1024)S(1)}, s32[4096]{0:T(1024)}, u32[]{:S(2)}) %copy-start.4) | copy-done | bytes 16408
  2.2 4.1 %collective-permute-start = (bf16[8,4096]{1,0:T(8,128)(2,1)S(1)}, bf16[8,4096]{1,0:T(8,128)(2,1)S(1)}, u32[]{:S(2)}, u32[]{:S(2)}) collective-permute-start(bf16[8,4096]{1,0:T(8,128)(2,1)S(1)} %weigh.1), channel_id=1, source_target_pairs={{0,4},{1,5},{2,6},{3,7},{4,0},{5,1},{6,2},{7,3},{8,12},{9,13},{10,... | collective-permute-start | bytes 196616 | tf_op jit(solution)/shard_map/ppermute | solution.py:20
  6.4 1.5 %collective-permute-start.6 = (bf16[8,4096]{1,0:T(8,128)(2,1)S(1)}, bf16[8,4096]{1,0:T(8,128)(2,1)S(1)}, u32[]{:S(2)}, u32[]{:S(2)}) collective-permute-start(bf16[8,4096]{1,0:T(8,128)(2,1)S(1)} %weigh.1), channel_id=1, source_target_pairs={{0,1},{1,0},{2,3},{3,2},{4,5},{5,4},{6,7},{7,6},{8,9},{9,8},{10,11... | collective-permute-start | bytes 196616 | tf_op jit(solution)/shard_map/ppermute | solution.py:20
  7.9 1.6 %collective-permute-start.1 = (bf16[8,4096]{1,0:T(8,128)(2,1)S(1)}, bf16[8,4096]{1,0:T(8,128)(2,1)S(1)}, u32[]{:S(2)}, u32[]{:S(2)}) collective-permute-start(bf16[8,4096]{1,0:T(8,128)(2,1)S(1)} %weigh.1), channel_id=1, source_target_pairs={{0,2},{1,3},{2,0},{3,1},{4,6},{5,7},{6,4},{7,5},{8,10},{9,11},{10,... | collective-permute-start | bytes 196616 | tf_op jit(solution)/shard_map/ppermute | solution.py:20
  9.9 0.4 collective-permute-start.14
  10.4 1.6 %collective-permute-start.2 = (bf16[8,4096]{1,0:T(8,128)(2,1)S(1)}, bf16[8,4096]{1,0:T(8,128)(2,1)S(1)}, u32[]{:S(2)}, u32[]{:S(2)}) collective-permute-start(bf16[8,4096]{1,0:T(8,128)(2,1)S(1)} %collective-permute-done), channel_id=1, source_target_pairs={{0,2},{1,3},{2,0},{3,1},{4,6},{5,7},{6,4},{7,5},{8,10},{9,11},{10,... | collective-permute-start | bytes 196616 | tf_op jit(solution)/shard_map/ppermute | solution.py:20
  11.9 1.6 %collective-permute-start.7 = (bf16[8,4096]{1,0:T(8,128)(2,1)S(1)}, bf16[8,4096]{1,0:T(8,128)(2,1)S(1)}, u32[]{:S(2)}, u32[]{:S(2)}) collective-permute-start(bf16[8,4096]{1,0:T(8,128)(2,1)S(1)} %collective-permute-done.6), channel_id=1, source_target_pairs={{0,16},{8,24},{16,0},{24,8},{1,17},{9,25},{17,1},{25,9},{2,18},{10... | collective-permute-start | bytes 196616 | tf_op jit(solution)/shard_map/ppermute | solution.py:20
  13.5 2.5 %collective-permute-done.13 = bf16[368,128]{1,0:T(8,128)(2,1)S(1)} collective-permute-done((bf16[368,128]{1,0:T(8,128)(2,1)S(1)}, bf16[368,128]{1,0:T(8,128)(2,1)S(1)}, u32[]{:S(2)}, u32[]{:S(2)}) %collective-permute-start.13) | collective-permute-done | bytes 94240 | tf_op jit(solution)/shard_map/ppermute | solution.py:20
  16.0 0.5 collective-permute-start.15
  16.5 1.8 %collective-permute-done.2 = bf16[8,4096]{1,0:T(8,128)(2,1)S(1)} collective-permute-done((bf16[8,4096]{1,0:T(8,128)(2,1)S(1)}, bf16[8,4096]{1,0:T(8,128)(2,1)S(1)}, u32[]{:S(2)}, u32[]{:S(2)}) %collective-permute-start.2) | collective-permute-done | bytes 65568 | tf_op jit(solution)/shard_map/ppermute | solution.py:20
  18.3 1.6 %collective-permute-start.4 = (bf16[32,4096]{1,0:T(8,128)(2,1)S(1)}, bf16[32,4096]{1,0:T(8,128)(2,1)S(1)}, u32[]{:S(2)}, u32[]{:S(2)}) collective-permute-start(bf16[32,4096]{1,0:T(8,128)(2,1)S(1)} %pad_maximum_fusion.1.refs_0_), channel_id=1, source_target_pairs={{0,16},{8,24},{16,0},{24,8},{1,17},{9,25},{17,1},{25,9},{2,18},{10... | collective-permute-start | bytes 786440 | tf_op jit(solution)/shard_map/ppermute | solution.py:20
  19.9 0.6 %collective-permute-start.9 = (bf16[24,4096]{1,0:T(8,128)(2,1)S(1)}, bf16[24,4096]{1,0:T(8,128)(2,1)S(1)}, u32[]{:S(2)}, u32[]{:S(2)}) collective-permute-start(bf16[24,4096]{1,0:T(8,128)(2,1)S(1)} %pad_maximum_fusion.2), channel_id=1, source_target_pairs={{0,1},{1,0},{2,3},{3,2},{4,5},{5,4},{6,7},{7,6},{8,9},{9,8},{10,11... | collective-permute-start | bytes 589832 | tf_op jit(solution)/shard_map/ppermute | solution.py:20
  20.5 5.4 %collective-permute-done.9.refs_6_ = bf16[24,4096]{1,0:T(8,128)(2,1)S(1)} collective-permute-done((bf16[24,4096]{1,0:T(8,128)(2,1)S(1)}, bf16[24,4096]{1,0:T(8,128)(2,1)S(1)}, u32[]{:S(2)}, u32[]{:S(2)}) %collective-permute-start.9) | collective-permute-done | bytes 196640 | tf_op jit(solution)/shard_map/ppermute | solution.py:20
  26.2 0.6 %collective-permute-start.16 = (bf16[1472,128]{1,0:T(8,128)(2,1)S(1)}, bf16[1472,128]{1,0:T(8,128)(2,1)S(1)}, u32[]{:S(2)}, u32[]{:S(2)}) collective-permute-start(bf16[1472,128]{1,0:T(8,128)(2,1)S(1)} %pad_maximum_fusion.refs_10_), channel_id=1, source_target_pairs={{0,1},{1,0},{2,3},{3,2},{4,5},{5,4},{6,7},{7,6},{8,9},{9,8},{10,11... | collective-permute-start | bytes 1130504 | tf_op jit(solution)/shard_map/ppermute | solution.py:20
  26.7 1.8 %plan.1.slot = s32[120]{0:T(128)S(1)} custom-call(s32[96]{0:T(128)S(1)} %bitcast.8), custom_call_target="tpu_custom_call" | custom-call | tf_op jit(solution)/shard_map/plan/pallas_call | solution.py:75
  29.8 2.1 %shard_map.95.refs_14_ = bf16[2,128,4096]{2,1,0:T(8,128)(2,1)S(1)} custom-call(s32[120]{0:T(128)S(1)} %plan.1.slot, bf16[3072,4096]{1,0:T(8,128)(2,1)S(1)} %copy-done, bf16[3072,128]{1,0:T(8,128)(2,1)S(1)} %copy-done.1), custom_call_target="tpu_custom_call" | custom-call | flops 939524096 | bytes 7340032 | tf_op jit(solution)/shard_map/pallas_call | solution.py:130
  32.0 0.5 collective-permute-start.10
  32.6 0.4 collective-permute-start.12
  33.0 5.1 %shard_map.96.refs_15_ = bf16[6,128,4096]{2,1,0:T(8,128)(2,1)S(1)} custom-call(s32[120]{0:T(128)S(1)} %plan.1.slot, bf16[3072,4096]{1,0:T(8,128)(2,1)S(1)} %copy-done, bf16[3072,128]{1,0:T(8,128)(2,1)S(1)} %copy-done.1), custom_call_target="tpu_custom_call" | custom-call | flops 2818572288 | bytes 22020096 | tf_op jit(solution)/shard_map/pallas_call | solution.py:130
  38.2 3.7 %meet.1 = f32[32,8,128]{2,1,0:T(8,128)} custom-call(bf16[32,4096]{1,0:T(8,128)(2,1)S(1)} %pad_maximum_fusion.1.refs_0_, bf16[32,4096]{1,0:T(8,128)(2,1)S(1)} %collective-permute-done.3.refs_1_, bf16[32,4096]{1,0:T(8,128)(2,1)S(1)} %collective-permute-done.4.refs_2_, bf16[32,4096]{1,0:T(8,128)(2,1)S(1)} %collective-permute-done.5.refs_3_, ...), custom_call_target="tpu_custom_call" | custom-call | flops 2147483648 | bytes 8388608 | tf_op jit(solution)/shard_map/meet/pallas_call | solution.py:357
  41.9 4.3 %all-to-all-start = ((f32[32,8,128]{2,1,0:T(8,128)}), f32[32,8,128]{2,1,0:T(8,128)S(1)}, u32[]{:S(2)}, u32[]{:S(2)}) async-start(f32[32,8,128]{2,1,0:T(8,128)} %meet.1), calls=%async_computation | async-start | bytes 262144 | tf_op jit(solution)/shard_map/all_to_all | solution.py:205
  46.2 7.8 %all-to-all-done.got = f32[32,8,128]{2,1,0:T(8,128)S(1)} async-done(((f32[32,8,128]{2,1,0:T(8,128)}), f32[32,8,128]{2,1,0:T(8,128)S(1)}, u32[]{:S(2)}, u32[]{:S(2)}) %all-to-all-start) | async-done | bytes 131104 | tf_op jit(solution)/shard_map/all_to_all | solution.py:205
  54.0 1.4 %gather_up.1 = (f32[1,128]{1,0:T(1,128)}, f32[49,8,64]{2,1,0:T(8,128)}) custom-call(f32[32,8,128]{2,1,0:T(8,128)S(1)} %all-to-all-done.got, s32[1,512]{1,0:T(1,128)S(1)} %iota_add_fusion.bins), custom_call_target="tpu_custom_call" | custom-call | tf_op jit(solution)/shard_map/gather_up/pallas_call | solution.py:253
  (38 shorter events, 1.0 us)
Async XLA Ops:
  1.5 0.7 %copy-start.4 = (s32[4096]{0:T(1024)S(1)}, s32[4096]{0:T(1024)}, u32[]{:S(2)}) copy-start(s32[4096]{0:T(1024)} %param.9) | copy-start | bytes 49156
  2.2 7.3 %copy-start.2 = (bf16[256,128]{1,0:T(8,128)(2,1)S(1)}, bf16[256,128]{1,0:T(8,128)(2,1)}, u32[]{:S(2)}) copy-start(bf16[256,128]{1,0:T(8,128)(2,1)} %slab.1) | copy-start | bytes 196612
  2.2 7.3 %copy-start.3 = (f32[49,128]{1,0:T(8,128)S(1)}, f32[49,128]{1,0:T(8,128)}, u32[]{:S(2)}) copy-start(f32[49,128]{1,0:T(8,128)} %mw.1) | copy-start | bytes 75268
  2.2 24.5 %copy-start.5 = (s32[96,1]{0,1:T(1,128)S(1)}, s32[96,1]{0,1:T(1,128)}, u32[]{:S(2)}) copy-start(s32[96,1]{0,1:T(1,128)} %param.10) | copy-start | bytes 1156
  2.2 27.6 %copy-start = (bf16[3072,4096]{1,0:T(8,128)(2,1)S(1)}, bf16[3072,4096]{1,0:T(8,128)(2,1)}, u32[]{:S(2)}) copy-start(bf16[3072,4096]{1,0:T(8,128)(2,1)} %orb.3) | copy-start | bytes 75497472
  2.2 27.6 %copy-start.1 = (bf16[3072,128]{1,0:T(8,128)(2,1)S(1)}, bf16[3072,128]{1,0:T(8,128)(2,1)}, u32[]{:S(2)}) copy-start(bf16[3072,128]{1,0:T(8,128)(2,1)} %phi.3) | copy-start | bytes 2359300
  2.2 8.1 %collective-permute-start = (bf16[8,4096]{1,0:T(8,128)(2,1)S(1)}, bf16[8,4096]{1,0:T(8,128)(2,1)S(1)}, u32[]{:S(2)}, u32[]{:S(2)}) collective-permute-start(bf16[8,4096]{1,0:T(8,128)(2,1)S(1)} %weigh.1), channel_id=1, source_target_pairs={{0,4},{1,5},{2,6},{3,7},{4,0},{5,1},{6,2},{7,3},{8,12},{9,13},{10,... | collective-permute-start | bytes 196616 | tf_op jit(solution)/shard_map/ppermute | solution.py:20
  6.4 5.6 %collective-permute-start.6 = (bf16[8,4096]{1,0:T(8,128)(2,1)S(1)}, bf16[8,4096]{1,0:T(8,128)(2,1)S(1)}, u32[]{:S(2)}, u32[]{:S(2)}) collective-permute-start(bf16[8,4096]{1,0:T(8,128)(2,1)S(1)} %weigh.1), channel_id=1, source_target_pairs={{0,1},{1,0},{2,3},{3,2},{4,5},{5,4},{6,7},{7,6},{8,9},{9,8},{10,11... | collective-permute-start | bytes 196616 | tf_op jit(solution)/shard_map/ppermute | solution.py:20
  7.9 8.6 %collective-permute-start.1 = (bf16[8,4096]{1,0:T(8,128)(2,1)S(1)}, bf16[8,4096]{1,0:T(8,128)(2,1)S(1)}, u32[]{:S(2)}, u32[]{:S(2)}) collective-permute-start(bf16[8,4096]{1,0:T(8,128)(2,1)S(1)} %weigh.1), channel_id=1, source_target_pairs={{0,2},{1,3},{2,0},{3,1},{4,6},{5,7},{6,4},{7,5},{8,10},{9,11},{10,... | collective-permute-start | bytes 196616 | tf_op jit(solution)/shard_map/ppermute | solution.py:20
  9.5 6.5 %collective-permute-start.13 = (bf16[368,128]{1,0:T(8,128)(2,1)S(1)}, bf16[368,128]{1,0:T(8,128)(2,1)S(1)}, u32[]{:S(2)}, u32[]{:S(2)}) collective-permute-start(bf16[368,128]{1,0:T(8,128)(2,1)S(1)} %pack.1), channel_id=1, source_target_pairs={{0,4},{1,5},{2,6},{3,7},{4,0},{5,1},{6,2},{7,3},{8,12},{9,13},{10,... | collective-permute-start | bytes 282632 | tf_op jit(solution)/shard_map/ppermute | solution.py:20
  9.9 16.2 %collective-permute-start.14 = (bf16[368,128]{1,0:T(8,128)(2,1)S(1)}, bf16[368,128]{1,0:T(8,128)(2,1)S(1)}, u32[]{:S(2)}, u32[]{:S(2)}) collective-permute-start(bf16[368,128]{1,0:T(8,128)(2,1)S(1)} %pack.1), channel_id=1, source_target_pairs={{0,2},{1,3},{2,0},{3,1},{4,6},{5,7},{6,4},{7,5},{8,10},{9,11},{10,... | collective-permute-start | bytes 282632 | tf_op jit(solution)/shard_map/ppermute | solution.py:20
  10.4 7.9 %collective-permute-start.2 = (bf16[8,4096]{1,0:T(8,128)(2,1)S(1)}, bf16[8,4096]{1,0:T(8,128)(2,1)S(1)}, u32[]{:S(2)}, u32[]{:S(2)}) collective-permute-start(bf16[8,4096]{1,0:T(8,128)(2,1)S(1)} %collective-permute-done), channel_id=1, source_target_pairs={{0,2},{1,3},{2,0},{3,1},{4,6},{5,7},{6,4},{7,5},{8,10},{9,11},{10,... | collective-permute-start | bytes 196616 | tf_op jit(solution)/shard_map/ppermute | solution.py:20
  11.9 8.5 %collective-permute-start.7 = (bf16[8,4096]{1,0:T(8,128)(2,1)S(1)}, bf16[8,4096]{1,0:T(8,128)(2,1)S(1)}, u32[]{:S(2)}, u32[]{:S(2)}) collective-permute-start(bf16[8,4096]{1,0:T(8,128)(2,1)S(1)} %collective-permute-done.6), channel_id=1, source_target_pairs={{0,16},{8,24},{16,0},{24,8},{1,17},{9,25},{17,1},{25,9},{2,18},{10... | collective-permute-start | bytes 196616 | tf_op jit(solution)/shard_map/ppermute | solution.py:20
  16.0 10.2 %collective-permute-start.15 = (bf16[368,128]{1,0:T(8,128)(2,1)S(1)}, bf16[368,128]{1,0:T(8,128)(2,1)S(1)}, u32[]{:S(2)}, u32[]{:S(2)}) collective-permute-start(bf16[368,128]{1,0:T(8,128)(2,1)S(1)} %collective-permute-done.13), channel_id=1, source_target_pairs={{0,2},{1,3},{2,0},{3,1},{4,6},{5,7},{6,4},{7,5},{8,10},{9,11},{10,... | collective-permute-start | bytes 282632 | tf_op jit(solution)/shard_map/ppermute | solution.py:20
  18.3 14.2 %collective-permute-start.4 = (bf16[32,4096]{1,0:T(8,128)(2,1)S(1)}, bf16[32,4096]{1,0:T(8,128)(2,1)S(1)}, u32[]{:S(2)}, u32[]{:S(2)}) collective-permute-start(bf16[32,4096]{1,0:T(8,128)(2,1)S(1)} %pad_maximum_fusion.1.refs_0_), channel_id=1, source_target_pairs={{0,16},{8,24},{16,0},{24,8},{1,17},{9,25},{17,1},{25,9},{2,18},{10... | collective-permute-start | bytes 786440 | tf_op jit(solution)/shard_map/ppermute | solution.py:20
  19.9 6.1 %collective-permute-start.9 = (bf16[24,4096]{1,0:T(8,128)(2,1)S(1)}, bf16[24,4096]{1,0:T(8,128)(2,1)S(1)}, u32[]{:S(2)}, u32[]{:S(2)}) collective-permute-start(bf16[24,4096]{1,0:T(8,128)(2,1)S(1)} %pad_maximum_fusion.2), channel_id=1, source_target_pairs={{0,1},{1,0},{2,3},{3,2},{4,5},{5,4},{6,7},{7,6},{8,9},{9,8},{10,11... | collective-permute-start | bytes 589832 | tf_op jit(solution)/shard_map/ppermute | solution.py:20
  20.4 11.5 %collective-permute-start.8 = (bf16[16,4096]{1,0:T(8,128)(2,1)S(1)}, bf16[16,4096]{1,0:T(8,128)(2,1)S(1)}, u32[]{:S(2)}, u32[]{:S(2)}) collective-permute-start(bf16[16,4096]{1,0:T(8,128)(2,1)S(1)} %constant_dynamic-update-slice_fusion.refs_4_), channel_id=1, source_target_pairs={{0,8},{8,0},{16,24},{24,16},{1,9},{9,1},{17,25},{25,17},{2,10},{10... | collective-permute-start | bytes 393224 | tf_op jit(solution)/shard_map/ppermute | solution.py:20
  25.9 6.6 %collective-permute-start.11 = (bf16[24,4096]{1,0:T(8,128)(2,1)S(1)}, bf16[24,4096]{1,0:T(8,128)(2,1)S(1)}, u32[]{:S(2)}, u32[]{:S(2)}) collective-permute-start(bf16[24,4096]{1,0:T(8,128)(2,1)S(1)} %collective-permute-done.9.refs_6_), channel_id=1, source_target_pairs={{0,16},{8,24},{16,0},{24,8},{1,17},{9,25},{17,1},{25,9},{2,18},{10... | collective-permute-start | bytes 589832 | tf_op jit(solution)/shard_map/ppermute | solution.py:20
  26.2 12.0 %collective-permute-start.16 = (bf16[1472,128]{1,0:T(8,128)(2,1)S(1)}, bf16[1472,128]{1,0:T(8,128)(2,1)S(1)}, u32[]{:S(2)}, u32[]{:S(2)}) collective-permute-start(bf16[1472,128]{1,0:T(8,128)(2,1)S(1)} %pad_maximum_fusion.refs_10_), channel_id=1, source_target_pairs={{0,1},{1,0},{2,3},{3,2},{4,5},{5,4},{6,7},{7,6},{8,9},{9,8},{10,11... | collective-permute-start | bytes 1130504 | tf_op jit(solution)/shard_map/ppermute | solution.py:20
  31.9 6.2 %collective-permute-start.3 = (bf16[32,4096]{1,0:T(8,128)(2,1)S(1)}, bf16[32,4096]{1,0:T(8,128)(2,1)S(1)}, u32[]{:S(2)}, u32[]{:S(2)}) collective-permute-start(bf16[32,4096]{1,0:T(8,128)(2,1)S(1)} %pad_maximum_fusion.1.refs_0_), channel_id=1, source_target_pairs={{0,8},{8,0},{16,24},{24,16},{1,9},{9,1},{17,25},{25,17},{2,10},{10... | collective-permute-start | bytes 786440 | tf_op jit(solution)/shard_map/ppermute | solution.py:20
  32.0 6.1 %collective-permute-start.10 = (bf16[24,4096]{1,0:T(8,128)(2,1)S(1)}, bf16[24,4096]{1,0:T(8,128)(2,1)S(1)}, u32[]{:S(2)}, u32[]{:S(2)}) collective-permute-start(bf16[24,4096]{1,0:T(8,128)(2,1)S(1)} %collective-permute-done.9.refs_6_), channel_id=1, source_target_pairs={{0,8},{8,0},{16,24},{24,16},{1,9},{9,1},{17,25},{25,17},{2,10},{10... | collective-permute-start | bytes 589832 | tf_op jit(solution)/shard_map/ppermute | solution.py:20
  32.5 5.7 %collective-permute-start.5 = (bf16[32,4096]{1,0:T(8,128)(2,1)S(1)}, bf16[32,4096]{1,0:T(8,128)(2,1)S(1)}, u32[]{:S(2)}, u32[]{:S(2)}) collective-permute-start(bf16[32,4096]{1,0:T(8,128)(2,1)S(1)} %collective-permute-done.4.refs_2_), channel_id=1, source_target_pairs={{0,8},{8,0},{16,24},{24,16},{1,9},{9,1},{17,25},{25,17},{2,10},{10... | collective-permute-start | bytes 786440 | tf_op jit(solution)/shard_map/ppermute | solution.py:20
  32.6 5.6 %collective-permute-start.12 = (bf16[24,4096]{1,0:T(8,128)(2,1)S(1)}, bf16[24,4096]{1,0:T(8,128)(2,1)S(1)}, u32[]{:S(2)}, u32[]{:S(2)}) collective-permute-start(bf16[24,4096]{1,0:T(8,128)(2,1)S(1)} %collective-permute-done.11.refs_8_), channel_id=1, source_target_pairs={{0,8},{8,0},{16,24},{24,16},{1,9},{9,1},{17,25},{25,17},{2,10},{10... | collective-permute-start | bytes 589832 | tf_op jit(solution)/shard_map/ppermute | solution.py:20
  41.9 12.1 %all-to-all-start = ((f32[32,8,128]{2,1,0:T(8,128)}), f32[32,8,128]{2,1,0:T(8,128)S(1)}, u32[]{:S(2)}, u32[]{:S(2)}) async-start(f32[32,8,128]{2,1,0:T(8,128)} %meet.1), calls=%async_computation | async-start | bytes 262144 | tf_op jit(solution)/shard_map/all_to_all | solution.py:205
